TPU v7x, 32 devices: a whole 2x2x4 slice. The times are simulated.
32 devices in a mesh: ya: 8 (over z, y), zb: 4 (over x, core).
Axes of the slice: x: 2, y: 2, z: 4, core: 2. Of those that a mesh axis runs over, the one named last changes fastest.
Arguments:
- source: float32 [128, 128, 512], P(None, 'ya', 'zb'), may hold values from -6 to 6
- symbol_x: float32 [128], replicated, may hold values from 0.3 to 3
- symbol_y: float32 [128], replicated, may hold values from 0.3 to 3
- symbol_z: float32 [512], replicated, may hold values from 0.3 to 3
Outputs:
- modes: float32 [128, 128, 512], P('ya', 'zb')
All inputs are finite; a program needn't handle non-finite values.
Results may differ from a plain program's by a relative error of at most 0.000071.
Values sent between devices are 32-bit elements; how exact they have to be, the bound alone decides.
A program may use at most 64 MiB of HBM per device.

v0:
```python
import jax
import jax.numpy as jnp
from jax import lax
from jax.sharding import PartitionSpec as P


def transform_table(count):
    rank = jnp.arange(count)
    angle = (
        jnp.pi
        / (count + 1)
        * ((rank[:, None] + 1) * (rank[None, :] + 1) % (2 * count + 2)).astype(jnp.float32)
    )
    return jnp.sin(angle) * (2.0 / (count + 1)) ** 0.5


def transform_dim(values, dim):
    moved = jnp.tensordot(
        values,
        transform_table(values.shape[dim]),
        axes=([dim], [0]),
        precision=lax.Precision.HIGHEST,
    )
    return jnp.moveaxis(moved, -1, dim)


def body(source, symbol_x, symbol_y, symbol_z):
    part_values = source
    part_values = transform_dim(part_values, 0)
    part_values = lax.all_to_all(part_values, "ya", split_axis=0, concat_axis=1, tiled=True)
    part_values = transform_dim(part_values, 1)
    pencil_values = part_values
    pencil_values = lax.all_to_all(pencil_values, "zb", split_axis=1, concat_axis=2, tiled=True)
    pencil_values = transform_dim(pencil_values, 2)
    share_x = pencil_values.shape[0]
    part_x = lax.dynamic_slice_in_dim(symbol_x, lax.axis_index("ya") * share_x, share_x)
    share_y = pencil_values.shape[1]
    part_y = lax.dynamic_slice_in_dim(symbol_y, lax.axis_index("zb") * share_y, share_y)
    symbol = part_x[:, None, None] + part_y[None, :, None] + symbol_z[None, None, :]
    pencil_values = pencil_values * lax.rsqrt(symbol)
    return pencil_values


def solution(mesh):
    placed = (P(None, "ya", "zb"), P(), P(), P())
    return jax.shard_map(
        body, mesh=mesh, in_specs=placed, out_specs=P("ya", "zb", None), check_vma=False
    )
```

profile of v0, /device:TPU:0, one launch (start us, length us, event | category | flops | bytes accessed | tf_op | source)
XLA Modules:
  0.0 66.0 jit_solution(8343601692508259223)
XLA Ops:
  0.0 0.0 copy-start
  0.0 1.2 %copy-done = f32[128,16,128]{2,1,0:T(8,128)S(1)} copy-done((f32[128,16,128]{2,1,0:T(8,128)S(1)}, f32[128,16,128]{2,1,0:T(8,128)}, u32[]{:S(2)}) %copy-start) | copy-done | bytes 1048600
  1.2 1.6 %fusion.6 = f32[128,16,128]{2,0,1:T(8,128)S(1)} fusion(f32[128,16,128]{2,1,0:T(8,128)S(1)} %copy-done, s32[128]{0:T(128)S(1)} %iota_add_fusion.1), kind=kOutput, calls=%fused_computation.8 | convolution fusion | flops 402817024 | bytes 2097664 | tf_op jit(solution)/shard_map/dot_general | solution.py:18
  2.8 0.6 copy.24
  3.5 32.9 %all_to_all.36 = f32[128,16,128]{2,1,0:T(8,128)S(1)} all-to-all(f32[128,16,128]{2,1,0:T(8,128)S(1)} %copy.24), channel_id=1, replica_groups=mesh['ya'=8,'zb'=4] {'ya'}, dimensions={0} | all-to-all | bytes 2097152 | tf_op jit(solution)/shard_map/all_to_all | solution.py:30
  36.3 0.1 copy.25
  36.4 2.0 %convolution_bitcast_fusion = f32[16,128,128]{1,2,0:T(8,128)S(1)} fusion(f32[16,128,128]{2,1,0:T(8,128)S(1)} %bitcast.21, s32[128]{0:T(128)S(1)} %iota_add_fusion.1), kind=kOutput, calls=%fused_computation.2 | convolution fusion | flops 402817024 | bytes 2097664 | tf_op jit(solution)/shard_map/dot_general | solution.py:18
  38.4 1.4 %copy.27 = f32[16,128,128]{2,0,1:T(8,128)} copy(f32[16,128,128]{1,2,0:T(8,128)S(1)} %convolution_bitcast_fusion) | data formatting | bytes 2097152 | tf_op jit(solution)/shard_map/transpose | solution.py:24
  39.8 3.7 %all-to-all-start.1 = ((f32[16,128,128]{2,0,1:T(8,128)}), f32[16,128,128]{2,0,1:T(8,128)S(1)}, u32[]{:S(2)}, u32[]{:S(2)}) async-start(f32[16,128,128]{2,0,1:T(8,128)} %copy.27), calls=%async_computation.1 | async-start | bytes 2097152 | tf_op jit(solution)/shard_map/all_to_all | solution.py:33
  43.5 0.0 copy-start.2
  43.5 0.6 copy-done.2
  44.2 0.1 dynamic_slice.7
  44.2 0.0 copy-start.3
  44.2 0.7 copy-done.3
  44.9 0.1 dynamic_slice.6
  45.0 0.1 broadcast_add_fusion
  45.0 12.7 %all-to-all-done.1 = f32[16,128,128]{2,0,1:T(8,128)S(1)} async-done(((f32[16,128,128]{2,0,1:T(8,128)}), f32[16,128,128]{2,0,1:T(8,128)S(1)}, u32[]{:S(2)}, u32[]{:S(2)}) %all-to-all-start.1) | async-done | bytes 1048608 | tf_op jit(solution)/shard_map/all_to_all | solution.py:33
  57.7 0.7 %copy.29 = f32[16,32,4,128]{3,2,1,0:T(4,128)S(1)} copy(f32[16,32,4,128]{3,0,1,2:T(8,128)S(1)} %bitcast.19) | data formatting | bytes 2097152 | tf_op jit(solution)/shard_map/all_to_all | solution.py:33
  58.4 0.0 copy-start.1
  58.4 0.4 all_to_all.33
  58.8 0.2 copy-done.1
  59.1 6.9 %convolution_multiply_fusion = f32[16,32,512]{2,1,0:T(8,128)} fusion(f32[16,32,512]{2,1,0:T(8,128)S(1)} %all_to_all.33, f32[512]{0:T(512)S(1)} %copy-done.1, f32[16,32]{1,0:T(8,128)S(1)} %broadcast_add_fusion, s32[512]{0:T(512)S(1)} %iota_add_fusion), kind=kOutput, calls=%fused_computation.1 | convolution fusion | flops 1613758464 | bytes 2103296 | tf_op jit(solution)/shard_map/dot_general | solution.py:18
  (2 shorter events, 0.0 us)
Async XLA Ops:
  0.0 1.2 %copy-start = (f32[128,16,128]{2,1,0:T(8,128)S(1)}, f32[128,16,128]{2,1,0:T(8,128)}, u32[]{:S(2)}) copy-start(f32[128,16,128]{2,1,0:T(8,128)} %param.4) | copy-start | bytes 3145732
  39.8 17.9 %all-to-all-start.1 = ((f32[16,128,128]{2,0,1:T(8,128)}), f32[16,128,128]{2,0,1:T(8,128)S(1)}, u32[]{:S(2)}, u32[]{:S(2)}) async-start(f32[16,128,128]{2,0,1:T(8,128)} %copy.27), calls=%async_computation.1 | async-start | bytes 2097152 | tf_op jit(solution)/shard_map/all_to_all | solution.py:33
  43.5 0.7 copy-start.2
  44.2 0.7 copy-start.3
  58.4 0.7 %copy-start.1 = (f32[512]{0:T(512)S(1)}, f32[512]{0:T(512)}, u32[]{:S(2)}) copy-start(f32[512]{0:T(512)} %param.7) | copy-start | bytes 6148
where the time goes:
time: 66.3 us; the launch traced here: 66 us
  blocking collectives  32.9 us (50%)
  waiting for transfers between devices  12.7 us (19%)
  matrix products  10.5 us (16%)
  local copies, waits for them, and re-layouts  6.11 us (9%)
  starting transfers between devices  3.7 us (6%)
    all_to_all x1, blocking collectives, body(): lax.all_to_all(part_values, 'ya', split_axis=0, concat_axis=1, tiled=True)  32.9 us
    all_to_all x1, waiting for transfers between devices, body(): lax.all_to_all(pencil_values, 'zb', split_axis=1, concat_axis=2, tiled=True)  12.7 us
    dot_general x3, matrix products, transform_dim(): jnp.tensordot(values, transform_table(values.shape[dim]), axes=([dim], [0...  10.5 us
    all_to_all x1, starting transfers between devices, body(): lax.all_to_all(pencil_values, 'zb', split_axis=1, concat_axis=2, tiled=True)  3.7 us
    unnamed x8, local copies, waits for them, and re-layouts  2.77 us
    transpose x1, local copies, waits for them, and re-layouts, transform_dim(): return jnp.moveaxis(moved, -1, dim)  1.38 us
  transfers between devices with their start and end apart: 1, of which 1 were waited for; matrix products, arithmetic and copies ran while one was open for 0% of the time, Pallas kernels for 0%

commit v1 on v0

--- a/solution.py
+++ b/solution.py
@@ -30,7 +30,12 @@
     part_values = lax.all_to_all(part_values, "ya", split_axis=0, concat_axis=1, tiled=True)
     part_values = transform_dim(part_values, 1)
     pencil_values = part_values
-    pencil_values = lax.all_to_all(pencil_values, "zb", split_axis=1, concat_axis=2, tiled=True)
+    pencil_values = jnp.concatenate(
+        lax.all_to_all(
+            jnp.stack(jnp.split(pencil_values, lax.axis_size("zb"), axis=1)), "zb", 0, 0
+        ),
+        axis=2,
+    )
     pencil_values = transform_dim(pencil_values, 2)
     share_x = pencil_values.shape[0]
     part_x = lax.dynamic_slice_in_dim(symbol_x, lax.axis_index("ya") * share_x, share_x)

time: 66.3 us -> 64.1 us (0.967)
  local copies, waits for them, and re-layouts: 6.11 us -> 3.48 us
  other arithmetic: 0.08 us -> 1.12 us
    transpose x1 -> x0, local copies, waits for them, and re-layouts: 1.38 us -> none  [transform_dim(): return jnp.moveaxis(moved, -1, dim)]
    all_to_all x2 -> x0, local copies, waits for them, and re-layouts: 1.1 us -> none  [body(): lax.all_to_all(pencil_values, 'zb', split_axis=1, concat_axis=2, tiled=True)]
    another operation x0 -> x1, other arithmetic: none -> 1.04 us  [body(): jnp.stack(jnp.split(pencil_values, lax.axis_size('zb'), axis=1))]
where the time goes in v1:
time: 64.1 us; the launch traced here: 63.8 us
  blocking collectives  32.9 us (51%)
  waiting for transfers between devices  12.9 us (20%)
  matrix products  9.9 us (15%)
  starting transfers between devices  3.52 us (5%)
  local copies, waits for them, and re-layouts  3.48 us (5%)
  other arithmetic  1.12 us (2%)
    all_to_all x1, blocking collectives, body(): lax.all_to_all(part_values, 'ya', split_axis=0, concat_axis=1, tiled=True)  32.9 us
    all_to_all x1, waiting for transfers between devices, body(): lax.all_to_all(jnp.stack(jnp.split(pencil_values, lax.axis_size('zb'), ax...  12.9 us
    dot_general x3, matrix products, transform_dim(): jnp.tensordot(values, transform_table(values.shape[dim]), axes=([dim], [0...  9.9 us
    all_to_all x1, starting transfers between devices, body(): lax.all_to_all(jnp.stack(jnp.split(pencil_values, lax.axis_size('zb'), ax...  3.52 us
    unnamed x8, local copies, waits for them, and re-layouts  2.53 us
  transfers between devices with their start and end apart: 1, of which 1 were waited for; matrix products, arithmetic and copies ran while one was open for 0% of the time, Pallas kernels for 0%

profile of v1, /device:TPU:0, one launch (start us, length us, event | category | flops | bytes accessed | tf_op | source)
XLA Modules:
  0.0 63.8 jit_solution(213104408088966404)
XLA Ops:
  0.0 0.0 copy-start
  0.0 1.2 %copy-done = f32[128,16,128]{2,1,0:T(8,128)S(1)} copy-done((f32[128,16,128]{2,1,0:T(8,128)S(1)}, f32[128,16,128]{2,1,0:T(8,128)}, u32[]{:S(2)}) %copy-start) | copy-done | bytes 1048600
  1.2 1.6 %fusion.8 = f32[128,16,128]{2,0,1:T(8,128)S(1)} fusion(f32[128,16,128]{2,1,0:T(8,128)S(1)} %copy-done, s32[128]{0:T(128)S(1)} %iota_add_fusion.1), kind=kOutput, calls=%fused_computation.11 | convolution fusion | flops 402817024 | bytes 2097664 | tf_op jit(solution)/shard_map/dot_general | solution.py:18
  2.8 0.6 copy.11
  3.4 32.9 %all_to_all.23 = f32[128,16,128]{2,1,0:T(8,128)S(1)} all-to-all(f32[128,16,128]{2,1,0:T(8,128)S(1)} %copy.11), channel_id=1, replica_groups=mesh['ya'=8,'zb'=4] {'ya'}, dimensions={0} | all-to-all | bytes 2097152 | tf_op jit(solution)/shard_map/all_to_all | solution.py:30
  36.3 0.1 copy.12
  36.4 1.4 %convolution_bitcast_fusion = f32[16,128,128]{2,1,0:T(8,128)S(1)} fusion(f32[16,128,128]{2,1,0:T(8,128)S(1)} %bitcast.31, s32[128]{0:T(128)S(1)} %iota_add_fusion.1), kind=kOutput, calls=%fused_computation.2 | convolution fusion | flops 402817024 | bytes 2097664 | tf_op jit(solution)/shard_map/dot_general | solution.py:18
  37.9 0.1 slice_bitcast_fusion.3
  38.0 1.0 %pad_maximum_fusion = f32[4,16,32,128]{3,2,1,0:T(8,128)} fusion(f32[1,16,32,128]{3,2,1,0:T(8,128)S(1)} %get-tuple-element.6, f32[1,16,32,128]{3,2,1,0:T(8,128)S(1)} %get-tuple-element.7, f32[1,16,32,128]{3,2,1,0:T(8,128)S(1)} %get-tuple-element.8, f32[1,16,32,128]{3,2,1,0:T(8,128)S(1)} %get-tuple-element.5), kind=kLoop, calls=%fused_computation.10 | loop fusion | flops 786432 | bytes 2097152 | tf_op jit(solution)/shard_map/stack | solution.py:35
  39.0 3.5 %all-to-all-start.1 = ((f32[4,16,32,128]{3,2,1,0:T(8,128)}), f32[4,16,32,128]{3,2,1,0:T(8,128)S(1)}, u32[]{:S(2)}, u32[]{:S(2)}) async-start(f32[4,16,32,128]{3,2,1,0:T(8,128)} %pad_maximum_fusion), calls=%async_computation.1 | async-start | bytes 2097152 | tf_op jit(solution)/shard_map/all_to_all | solution.py:34
  42.5 0.0 copy-start.2
  42.5 0.6 %copy-done.2 = f32[128]{0:T(128)S(1)} copy-done((f32[128]{0:T(128)S(1)}, f32[128]{0:T(128)}, u32[]{:S(2)}) %copy-start.2) | copy-done | bytes 536
  43.2 0.1 dynamic_slice.6
  43.3 0.0 copy-start.3
  43.3 0.7 %copy-done.3 = f32[128]{0:T(128)S(1)} copy-done((f32[128]{0:T(128)S(1)}, f32[128]{0:T(128)}, u32[]{:S(2)}) %copy-start.3) | copy-done | bytes 536
  43.9 0.1 dynamic_slice.7
  44.0 0.0 copy-start.1
  44.0 0.1 broadcast_add_fusion
  44.1 12.9 %all-to-all-done.1 = f32[4,16,32,128]{3,2,1,0:T(8,128)S(1)} async-done(((f32[4,16,32,128]{3,2,1,0:T(8,128)}), f32[4,16,32,128]{3,2,1,0:T(8,128)S(1)}, u32[]{:S(2)}, u32[]{:S(2)}) %all-to-all-start.1) | async-done | bytes 1048608 | tf_op jit(solution)/shard_map/all_to_all | solution.py:34
  56.9 0.0 copy-done.1
  56.9 6.9 %convolution_multiply_fusion = f32[16,32,512]{2,1,0:T(8,128)} fusion(f32[512]{0:T(512)S(1)} %copy-done.1, f32[16,32]{1,0:T(8,128)S(1)} %broadcast_add_fusion, s32[512]{0:T(512)S(1)} %iota_add_fusion, f32[4,16,32,128]{3,2,1,0:T(8,128)S(1)} %all-to-all-done.1), kind=kOutput, calls=%fused_computation.1 | convolution fusion | flops 1613758464 | bytes 2103296 | tf_op jit(solution)/shard_map/dot_general | solution.py:18
  (2 shorter events, 0.0 us)
Async XLA Ops:
  0.0 1.2 %copy-start = (f32[128,16,128]{2,1,0:T(8,128)S(1)}, f32[128,16,128]{2,1,0:T(8,128)}, u32[]{:S(2)}) copy-start(f32[128,16,128]{2,1,0:T(8,128)} %param.4) | copy-start | bytes 3145732
  39.0 17.9 %all-to-all-start.1 = ((f32[4,16,32,128]{3,2,1,0:T(8,128)}), f32[4,16,32,128]{3,2,1,0:T(8,128)S(1)}, u32[]{:S(2)}, u32[]{:S(2)}) async-start(f32[4,16,32,128]{3,2,1,0:T(8,128)} %pad_maximum_fusion), calls=%async_computation.1 | async-start | bytes 2097152 | tf_op jit(solution)/shard_map/all_to_all | solution.py:34
  42.5 0.7 %copy-start.2 = (f32[128]{0:T(128)S(1)}, f32[128]{0:T(128)}, u32[]{:S(2)}) copy-start(f32[128]{0:T(128)} %param.5) | copy-start | bytes 1540
  43.3 0.7 %copy-start.3 = (f32[128]{0:T(128)S(1)}, f32[128]{0:T(128)}, u32[]{:S(2)}) copy-start(f32[128]{0:T(128)} %param.6) | copy-start | bytes 1540
  44.0 12.9 %copy-start.1 = (f32[512]{0:T(512)S(1)}, f32[512]{0:T(512)}, u32[]{:S(2)}) copy-start(f32[512]{0:T(512)} %param.7) | copy-start | bytes 6148
